TPU v7x, 32 devices: a whole 2x2x4 slice. The times are simulated.
32 devices in a mesh: section: 2 (over core), mp: 4 (over y, x), dp: 4 (over z).
Axes of the slice: x: 2, y: 2, z: 4, core: 2. Of those that a mesh axis runs over, the one named last changes fastest.
Arguments:
- value_grad: bfloat16 [2, 2048, 3072], P('section', 'dp', 'mp'), may hold values from -6 to 6
- stream: bfloat16 [2, 2048, 3072], P('section', 'dp'), may hold values from -300 to 300
- weights: bfloat16 [2, 3072, 3072], P('section', 'mp'), may hold values from -0.109375 to 0.109375
- gain: float32 [2, 3072], P('section'), may hold values from 0.25 to 1.75
- top_grad: bfloat16 [2048, 3072], P('dp'), may hold values from -6 to 6
- counts: int32 [4], P('dp'), may hold values from 1 to 2, as said below
Outputs:
- weight_grad: bfloat16 [2, 3072, 3072], P('section', ('mp', 'dp'))
- residual_grad: bfloat16 [2, 2048, 3072], P('section', 'dp', 'mp')
Inputs may be any that keep to these rules, and one draw needn't show every extreme that they name: counts[r] counts the live micro-batches of replica r; some replica has all 2.
All inputs are finite; a program needn't handle non-finite values.
Results may differ from a plain program's by a relative error of at most 0.009.
Values may be sent and summed in bfloat16 or wider, within the bound.
A program may use at most 64 MiB of HBM per device.

v0:
```python
import jax
import jax.numpy as jnp
from jax import lax
from jax.sharding import PartitionSpec as P

TOK_MB = 256


def shifted(value, axis, by):
    peers = lax.axis_size(axis)
    pairs = [(i, i + by) for i in range(peers) if 0 <= i + by < peers]
    return lax.ppermute(value, axis, pairs)


def normalize(stream_rows):
    values = stream_rows.astype(jnp.float32)
    average = jnp.mean(values, axis=-1, keepdims=True)
    centred = values - average
    variance = jnp.mean(centred * centred, axis=-1, keepdims=True)
    inv_scale = lax.rsqrt(variance + 1e-06)
    return (centred * inv_scale, inv_scale)


def shards(value_grad, stream, weights, gain, top_grad, counts):
    section_index = lax.axis_index("section")
    model_index = lax.axis_index("mp")
    row_total = stream.shape[1]
    whitened, inv_scale = normalize(stream[0])
    gain_row = gain[0]
    normed = (whitened * gain_row).astype(jnp.bfloat16)
    micro_index = jnp.arange(row_total, dtype=jnp.int32) // TOK_MB
    live_mask = (micro_index < counts[0]).astype(jnp.bfloat16)
    masked = value_grad[0] * live_mask[:, None]
    grad_rows = lax.psum_scatter(
        lax.dot_general(
            masked, normed, (((0,), (0,)), ((), ())), preferred_element_type=jnp.float32
        ),
        "dp",
        scatter_dimension=0,
        tiled=True,
    )
    weight_grad = grad_rows.astype(jnp.bfloat16)[None]
    partial_sum = jnp.dot(value_grad[0], weights[0], preferred_element_type=jnp.float32)
    width = whitened.shape[1]
    share_width = width // lax.axis_size("mp")
    first_col = model_index * share_width
    norm_grad = lax.psum(partial_sum.astype(jnp.bfloat16), "mp").astype(jnp.float32)
    scaled_grad = norm_grad * gain_row
    first_mean = jnp.mean(scaled_grad, axis=-1, keepdims=True)
    second_mean = jnp.mean(scaled_grad * whitened, axis=-1, keepdims=True)
    norm_back = inv_scale * (scaled_grad - first_mean - whitened * second_mean)
    above_grad = (top_grad.astype(jnp.float32) + norm_back).astype(jnp.bfloat16)
    below_grad = shifted(above_grad, "section", -1)
    lower_grad = (below_grad.astype(jnp.float32) + norm_back).astype(jnp.bfloat16)
    whole_grad = jnp.where(section_index == 0, lower_grad, above_grad)
    result = lax.dynamic_slice_in_dim(whole_grad, first_col, share_width, 1)
    return (weight_grad, result[None])


def solution(mesh):
    in_specs = (
        P("section", "dp", "mp"),
        P("section", "dp", None),
        P("section", "mp", None),
        P("section", None),
        P("dp", None),
        P("dp"),
    )
    out_specs = (P("section", ("mp", "dp"), None), P("section", "dp", "mp"))
    return jax.shard_map(shards, mesh=mesh, in_specs=in_specs, out_specs=out_specs, check_vma=False)
```

profile of v0, /device:TPU:0, one launch (start us, length us, event | category | flops | bytes accessed | tf_op | source)
XLA Modules:
  0.0 197.5 jit_solution(13738247779773954277)
XLA Ops:
  8.0 0.0 copy-start
  8.0 0.0 all-reduce.2.cloned.1.call-start
  8.1 7.0 %fusion.15 = bf16[512,3072]{1,0:T(8,128)(2,1)} fusion(bf16[1,768,3072]{2,1,0:T(8,128)(2,1)} %param.8, bf16[1,512,768]{2,1,0:T(8,128)(2,1)} %param.6), kind=kOutput, calls=%fused_computation.20 | convolution fusion | flops 2417491968 | bytes 8650752 | tf_op jit(solution)/shard_map/dot_general | solution.py:43
  15.1 0.0 copy-start.3
  15.1 0.0 all-reduce.2.cloned.1.call-update
  15.1 0.0 reduce-scatter.2.cloned.1.call-start
  15.1 0.0 copy-start.4
  15.9 0.0 copy-done
  15.9 0.5 convert_reduce_fusion
  16.4 1.0 fusion.11
  17.4 0.0 copy-done.3
  17.4 0.0 copy-done.4
  17.4 5.5 %fusion.19 = f32[768,3072]{1,0:T(8,128)} fusion(bf16[1,512,3072]{2,1,0:T(8,128)(2,1)S(1)} %copy-done, f32[3072]{0:T(1024)S(1)} %bitcast.42, f32[512]{0:T(512)S(1)} %add_rsqrt_fusion, f32[512]{0:T(512)S(1)} %broadcast_multiply_fusion.2, bf16[1,512,768]{2,1,0:T(8,128)(2,1)S(1)} %copy-done.4, bf16[512]{0:T(512)(128)(2,1)S(1)} %fusion.35), kind=kOutput, calls=%fused_computation.22 | convolution fusion | flops 2424176640 | bytes 13386752 | tf_op jit(solution)/shard_map/dot_general | solution.py:35
  22.9 0.0 reduce-scatter.2.cloned.1.call-update
  22.9 82.0 %all-reduce.2.cloned.1.call-done = bf16[512,3072]{1,0:T(8,128)(2,1)} async-done(((bf16[512,3072]{1,0:T(8,128)(2,1)}), bf16[512,3072]{1,0:T(8,128)(2,1)}) %all-reduce.2.cloned.1.call-update) | async-done | bytes 3145744 | tf_op jit(solution)/shard_map/psum | solution.py:47
  104.9 3.6 %fusion.12 = (f32[512]{0:T(512)S(1)}, f32[512]{0:T(512)S(1)}) fusion(bf16[512,3072]{1,0:T(8,128)(2,1)} %all-reduce.2.cloned.1.call-done, f32[3072]{0:T(1024)S(1)} %bitcast.43, f32[512]{0:T(512)S(1)} %add_rsqrt_fusion, f32[512]{0:T(512)S(1)} %broadcast_multiply_fusion.2, bf16[1,512,3072]{2,1,0:T(8,128)(2,1)S(1)} %copy-done), kind=kLoop, calls=%fused_computation.17 | loop fusion | flops 12581888 | bytes 6311936 | tf_op jit(solution)/shard_map/reduce_sum | solution.py:49
  108.5 0.0 copy-done.1
  108.5 0.3 copy-done.2
  108.8 6.0 %add_convert_fusion = (bf16[512,3072]{1,0:T(8,128)(2,1)}, f32[512,3072]{1,0:T(8,128)}) fusion(bf16[512,3072]{1,0:T(8,128)(2,1)S(1)} %copy-done.2, f32[512]{0:T(512)S(1)} %get-tuple-element.6, f32[512]{0:T(512)S(1)} %broadcast_multiply_fusion.2, bf16[1,512,3072]{2,1,0:T(8,128)(2,1)S(1)} %copy-done, f32[512]{0:T(512)S(1)} %get-tuple-element.7, ...), kind=kLoop, calls=%fused_computation.15 | loop fusion | flops 18874368 | bytes 18894848 | tf_op jit(solution)/shard_map/convert_element_type | solution.py:52
  114.8 1.3 collective-permute-start
  116.1 6.5 %collective-permute-done = bf16[512,3072]{1,0:T(8,128)(2,1)S(1)} collective-permute-done((bf16[512,3072]{1,0:T(8,128)(2,1)}, bf16[512,3072]{1,0:T(8,128)(2,1)S(1)}, u32[]{:S(2)}, u32[]{:S(2)}) %collective-permute-start) | collective-permute-done | bytes 3145760 | tf_op jit(solution)/shard_map/ppermute | solution.py:12
  122.6 2.8 %fusion.26 = bf16[1,512,768]{2,1,0:T(8,128)(2,1)} fusion(f32[512,3072]{1,0:T(8,128)} %get-tuple-element.5, s32[]{:T(128)S(6)} %select_n.23, bf16[512,3072]{1,0:T(8,128)(2,1)} %get-tuple-element.4, bf16[512,3072]{1,0:T(8,128)(2,1)S(1)} %collective-permute-done, pred[]{:T(512)S(6)} %eq.3), kind=kLoop, calls=%fused_computation.30 | loop fusion | flops 1572864 | bytes 3932165 | tf_op jit(solution)/shard_map/broadcast_in_dim | solution.py:57
  125.3 61.8 %reduce-scatter.2.cloned.1.call-done = f32[192,3072]{1,0:T(8,128)} async-done(((f32[768,3072]{1,0:T(8,128)}), f32[192,3072]{1,0:T(8,128)}) %reduce-scatter.2.cloned.1.call-update) | async-done | bytes 2359312 | tf_op jit(solution)/shard_map/reduce_scatter | solution.py:34
  187.2 2.8 %convert_bitcast_fusion.1 = bf16[1,192,3072]{2,1,0:T(8,128)(2,1)} fusion(f32[192,3072]{1,0:T(8,128)} %reduce-scatter.2.cloned.1.call-done), kind=kLoop, calls=%fused_computation.28 | loop fusion | flops 589824 | bytes 3538944 | tf_op jit(solution)/shard_map/broadcast_in_dim | solution.py:42
  (6 shorter events, 0.0 us)
Async XLA Ops:
  8.0 7.9 %copy-start = (bf16[1,512,3072]{2,1,0:T(8,128)(2,1)S(1)}, bf16[1,512,3072]{2,1,0:T(8,128)(2,1)}, u32[]{:S(2)}) copy-start(bf16[1,512,3072]{2,1,0:T(8,128)(2,1)} %param.7) | copy-start | bytes 9437188
  8.0 96.9 %all-reduce.2.cloned.1.call-start = ((), (), s32[]{:S(2)}) async-start(), calls=%async_computation.2 | async-start | bytes 6291456 | tf_op jit(solution)/shard_map/psum | solution.py:47
  15.1 2.3 %copy-start.3 = (f32[1,3072]{1,0:T(1,128)S(1)}, f32[1,3072]{1,0:T(1,128)}, u32[]{:S(2)}) copy-start(f32[1,3072]{1,0:T(1,128)} %param.9) | copy-start | bytes 36868
  15.1 172.1 %reduce-scatter.2.cloned.1.call-start = ((), (), s32[]{:S(2)}) async-start(), calls=%async_computation.1 | async-start | bytes 11796480 | tf_op jit(solution)/shard_map/reduce_scatter | solution.py:34
  15.1 2.2 %copy-start.4 = (bf16[1,512,768]{2,1,0:T(8,128)(2,1)S(1)}, bf16[1,512,768]{2,1,0:T(8,128)(2,1)}, u32[]{:S(2)}) copy-start(bf16[1,512,768]{2,1,0:T(8,128)(2,1)} %param.6) | copy-start | bytes 2359300
  104.9 3.6 %copy-start.1 = (bf16[512,3072]{1,0:T(8,128)(2,1)S(1)}, bf16[512,3072]{1,0:T(8,128)(2,1)}, u32[]{:S(2)}) copy-start(bf16[512,3072]{1,0:T(8,128)(2,1)} %all-reduce.2.cloned.1.call-done) | copy-start | bytes 9437188
  104.9 3.9 %copy-start.2 = (bf16[512,3072]{1,0:T(8,128)(2,1)S(1)}, bf16[512,3072]{1,0:T(8,128)(2,1)}, u32[]{:S(2)}) copy-start(bf16[512,3072]{1,0:T(8,128)(2,1)} %param.10) | copy-start | bytes 9437188
  114.8 7.8 %collective-permute-start = (bf16[512,3072]{1,0:T(8,128)(2,1)}, bf16[512,3072]{1,0:T(8,128)(2,1)S(1)}, u32[]{:S(2)}, u32[]{:S(2)}) collective-permute-start(bf16[512,3072]{1,0:T(8,128)(2,1)} %get-tuple-element.4), channel_id=1, source_target_pairs={{16,0},{17,1},{18,2},{19,3},{20,4},{21,5},{22,6},{23,7},{24,8},{25... | collective-permute-start | bytes 9437192 | tf_op jit(solution)/shard_map/ppermute | solution.py:12
Sparse Core Ops, SparseCore 0:
  15.2 89.6 all-reduce.1
Sparse Core Ops, SparseCore 1:
  23.0 164.1 reduce-scatter.1
where the time goes:
time: 198 us; the launch traced here: 197 us
  waiting for transfers between devices  150 us (76%)
  other arithmetic  16.7 us (8%)
  between operations  16.3 us (8%)
  matrix products  12.5 us (6%)
    psum x1, waiting for transfers between devices, shards(): lax.psum(partial_sum.astype(jnp.bfloat16), 'mp').astype(jnp.float32)  82 us
    reduce_scatter x1, waiting for transfers between devices, shards(): lax.psum_scatter(lax.dot_general(masked, normed, (((0,), (0,)), ((), ()))...  61.8 us
    dot_general x1, matrix products, shards(): jnp.dot(value_grad[0], weights[0], preferred_element_type=jnp.float32)  7.01 us
    ppermute x1, waiting for transfers between devices, shifted(): return lax.ppermute(value, axis, pairs)  6.46 us
    convert_element_type x1, other arithmetic, shards(): above_grad = (top_grad.astype(jnp.float32) + norm_back).astype(jnp.bfloat16)  6 us
    dot_general x1, matrix products, shards(): lax.dot_general(masked, normed, (((0,), (0,)), ((), ())), preferred_eleme...  5.54 us
  transfers between devices with their start and end apart: 3, of which 3 were waited for; matrix products, arithmetic and copies ran while one was open for 10% of the time, Pallas kernels for 0%

commit v1 on v0

v1 whole, which is shorter than its diff:
```python
import jax
import jax.numpy as jnp
from jax import lax
from jax.sharding import PartitionSpec as P

TOK_MB = 256


def normalize(stream_rows):
    values = stream_rows.astype(jnp.float32)
    average = jnp.mean(values, axis=-1, keepdims=True)
    centred = values - average
    variance = jnp.mean(centred * centred, axis=-1, keepdims=True)
    inv_scale = lax.rsqrt(variance + 1e-06)
    return (centred * inv_scale, inv_scale)


def shards(value_grad, stream, weights, gain, top_grad, counts):
    section_index = lax.axis_index("section")
    model_index = lax.axis_index("mp")
    row_total = stream.shape[1]
    whitened, inv_scale = normalize(stream[0])
    gain_row = gain[0]
    width = whitened.shape[1]
    share = width // lax.axis_size("mp")
    first_col = model_index * share
    cols = lambda a: lax.dynamic_slice_in_dim(a, first_col, share, 1)
    partial = jnp.dot(value_grad[0], weights[0], preferred_element_type=jnp.float32)
    partial = partial.astype(jnp.bfloat16)
    local = partial.astype(jnp.float32) * gain_row
    sums = jnp.stack([jnp.sum(local, -1), jnp.sum(local * whitened, -1)])
    norm_grad = lax.psum_scatter(partial, "mp", scatter_dimension=1, tiled=True)
    sums = lax.psum(sums, "mp") * (1.0 / width)
    normed = (whitened * gain_row).astype(jnp.bfloat16)
    micro_index = jnp.arange(row_total, dtype=jnp.int32) // TOK_MB
    live_mask = (micro_index < counts[0]).astype(jnp.bfloat16)
    masked = value_grad[0] * live_mask[:, None]
    product = lax.dot_general(
        masked, normed, (((0,), (0,)), ((), ())), preferred_element_type=jnp.float32
    )
    weight_grad = lax.psum_scatter(
        product.astype(jnp.bfloat16), "dp", scatter_dimension=0, tiled=True
    )[None]
    scaled = norm_grad.astype(jnp.float32) * cols(gain)
    branch = inv_scale * (scaled - sums[0][:, None] - cols(whitened) * sums[1][:, None])
    above = (cols(top_grad).astype(jnp.float32) + branch).astype(jnp.bfloat16)
    below = lax.ppermute(above, "section", [(1, 0)])
    lower = (below.astype(jnp.float32) + branch).astype(jnp.bfloat16)
    result = jnp.where(section_index == 0, lower, above)
    return (weight_grad, result[None])


def solution(mesh):
    in_specs = (
        P("section", "dp", "mp"),
        P("section", "dp", None),
        P("section", "mp", None),
        P("section", None),
        P("dp", None),
        P("dp"),
    )
    out_specs = (P("section", ("mp", "dp"), None), P("section", "dp", "mp"))
    return jax.shard_map(shards, mesh=mesh, in_specs=in_specs, out_specs=out_specs, check_vma=False)
```

time: 198 us -> 162 us (0.82)
  waiting for transfers between devices: 150 us -> 110 us
  blocking collectives: 0 us -> 11.9 us
  other arithmetic: 16.7 us -> 9.15 us
    psum x1 -> x0, waiting for transfers between devices: 82 us -> none  [shards(): lax.psum(partial_sum.astype(jnp.bfloat16), 'mp').astype(jnp.float32)]
    reduce_scatter x1 -> x2, waiting for transfers between devices: 61.8 us -> 107 us  [the longest x1 78.4 us: shards(): lax.psum_scatter(product.astype(jnp.bfloat16), 'dp', scatter_dimension=0,...]
    psum x0 -> x1, blocking collectives: none -> 11.9 us  [shards(): sums = lax.psum(sums, 'mp') * (1.0 / width)]
    reduce_sum x1 -> x0, other arithmetic: 3.61 us -> none  [shards(): first_mean = jnp.mean(scaled_grad, axis=-1, keepdims=True)]
    convert_element_type x1, other arithmetic: 6 us -> 2.41 us  [shards(): above = (cols(top_grad).astype(jnp.float32) + branch).astype(jnp.bfloat16)]
    ppermute x1, waiting for transfers between devices: 6.46 us -> 2.87 us  [shards(): below = lax.ppermute(above, 'section', [(1, 0)])]
    broadcast_in_dim x1 -> x0, other arithmetic: 2.84 us -> none  [shards(): weight_grad = grad_rows.astype(jnp.bfloat16)[None]]
    reduce_sum x1, other arithmetic: 0.49 us -> 2.53 us  [normalize(): average = jnp.mean(values, axis=-1, keepdims=True)]
  transfers between devices with their start and end apart: 3 -> 3, of which waited for: 3 -> 3; matrix products, arithmetic and copies ran while one was open for 10% -> 7% of each run, Pallas kernels for 0% -> 0%
where the time goes in v1:
time: 162 us; the launch traced here: 161 us
  waiting for transfers between devices  110 us (68%)
  between operations  14.8 us (9%)
  matrix products  14.2 us (9%)
  blocking collectives  11.9 us (7%)
  other arithmetic  9.15 us (6%)
    reduce_scatter x1, waiting for transfers between devices, shards(): lax.psum_scatter(product.astype(jnp.bfloat16), 'dp', scatter_dimension=0,...  78.4 us
    reduce_scatter x1, waiting for transfers between devices, shards(): norm_grad = lax.psum_scatter(partial, 'mp', scatter_dimension=1, tiled=True)  28.3 us
    psum x1, blocking collectives, shards(): sums = lax.psum(sums, 'mp') * (1.0 / width)  11.9 us
    dot_general x1, matrix products, shards(): jnp.dot(value_grad[0], weights[0], preferred_element_type=jnp.float32)  8.28 us
    dot_general x1, matrix products, shards(): lax.dot_general(masked, normed, (((0,), (0,)), ((), ())), preferred_eleme...  5.96 us
  transfers between devices with their start and end apart: 3, of which 3 were waited for; matrix products, arithmetic and copies ran while one was open for 7% of the time, Pallas kernels for 0%

profile of v1, /device:TPU:0, one launch (start us, length us, event | category | flops | bytes accessed | tf_op | source)
XLA Modules:
  0.0 161.4 jit_solution(5336192532830619747)
XLA Ops:
  7.2 0.0 copy-start
  7.2 0.0 copy-start.2
  7.2 0.0 reduce-scatter.5.cloned.1.call-start
  7.2 0.0 copy-start.3
  7.2 2.5 %convert_reduce_fusion = f32[512]{0:T(512)S(1)} fusion(bf16[1,512,3072]{2,1,0:T(8,128)(2,1)} %param.7), kind=kLoop, calls=%fused_computation.2 | loop fusion | flops 3145216 | bytes 3147776 | tf_op jit(solution)/shard_map/reduce_sum | solution.py:11
  9.8 0.2 copy-done
  10.0 1.0 fusion.6
  11.0 0.0 copy-done.2
  11.0 0.0 copy-done.3
  11.0 8.3 %fusion.7 = (f32[512]{0:T(512)S(1)}, f32[512]{0:T(512)S(1)}, f32[512,3072]{1,0:T(8,128)}, bf16[512,3072]{1,0:T(8,128)(2,1)}) fusion(f32[3072]{0:T(1024)S(1)} %bitcast.46, f32[512]{0:T(512)S(1)} %add_rsqrt_fusion, f32[512]{0:T(512)S(1)} %broadcast_multiply_fusion.1, bf16[1,512,3072]{2,1,0:T(8,128)(2,1)S(1)} %copy-done, bf16[1,768,3072]{2,1,0:T(8,128)(2,1)} %param.8, ...), kind=kOutput, calls=%fused_computation.12 | convolution fusion | flops 2430073856 | bytes 18108416 | tf_op jit(solution)/shard_map/dot_general | solution.py:28
  19.3 0.0 reduce-scatter.5.cloned.1.call-update
  19.3 0.0 reduce-scatter.3.cloned.1.call-start
  20.0 6.0 %convolution_convert_fusion = bf16[768,3072]{1,0:T(8,128)(2,1)} fusion(bf16[1,512,3072]{2,1,0:T(8,128)(2,1)S(1)} %copy-done, f32[3072]{0:T(1024)S(1)} %bitcast.47, f32[512]{0:T(512)S(1)} %add_rsqrt_fusion, f32[512]{0:T(512)S(1)} %broadcast_multiply_fusion.1, bf16[1,512,768]{2,1,0:T(8,128)(2,1)} %param.6, bf16[512]{0:T(512)(128)(2,1)S(1)} %fusion.28), kind=kOutput, calls=%fused_computation.13 | convolution fusion | flops 2426535936 | bytes 8668160 | tf_op jit(solution)/shard_map/dot_general | solution.py:38
  26.0 0.0 reduce-scatter.3.cloned.1.call-update
  26.0 11.9 %psum.7 = f32[2,512]{1,0:T(2,128)S(1)} all-reduce(f32[2,512]{1,0:T(2,128)S(1)} %pad_maximum_fusion), channel_id=1, replica_groups=mesh['section'=2,'mp'=4,'dp'=4] {'mp'}, use_global_device_ids=true, to_apply=%region_6.7 | all-reduce | flops 1024 | bytes 8192 | tf_op jit(solution)/shard_map/psum | solution.py:33
  38.0 28.3 %reduce-scatter.5.cloned.1.call-done = bf16[512,768]{1,0:T(8,128)(2,1)} async-done(((bf16[512,3072]{1,0:T(8,128)(2,1)}), bf16[512,768]{1,0:T(8,128)(2,1)}) %reduce-scatter.5.cloned.1.call-update) | async-done | bytes 786448 | tf_op jit(solution)/shard_map/reduce_scatter | solution.py:32
  66.3 0.0 copy-start.1
  66.3 2.4 %add_convert_fusion.1 = bf16[512,768]{1,0:T(8,128)(2,1)S(1)} fusion(bf16[512,3072]{1,0:T(8,128)(2,1)} %param.10, s32[]{:T(128)S(6)} %select_n.24, f32[512]{0:T(512)S(1)} %bitcast.42, f32[512,3072]{1,0:T(8,128)} %get-tuple-element.4, f32[512]{0:T(512)S(1)} %bitcast.40, f32[768]{0:T(1024)S(1)} %dynamic-slice_reduce_fusion, ...), kind=kLoop, calls=%fused_computation.22 | loop fusion | flops 3538944 | bytes 3941380 | tf_op jit(solution)/shard_map/convert_element_type | solution.py:46
  68.7 1.3 collective-permute-start
  70.0 2.9 %collective-permute-done = bf16[512,768]{1,0:T(8,128)(2,1)S(1)} collective-permute-done((bf16[512,768]{1,0:T(8,128)(2,1)S(1)}, bf16[512,768]{1,0:T(8,128)(2,1)S(1)}, u32[]{:S(2)}, u32[]{:S(2)}) %collective-permute-start) | collective-permute-done | bytes 786464 | tf_op jit(solution)/shard_map/ppermute | solution.py:47
  72.9 0.0 copy-done.1
  72.9 3.2 %fusion.19 = bf16[1,512,768]{2,1,0:T(8,128)(2,1)} fusion(bf16[512,768]{1,0:T(8,128)(2,1)S(1)} %add_convert_fusion.1, bf16[512,768]{1,0:T(8,128)(2,1)S(1)} %collective-permute-done, pred[]{:T(512)S(6)} %eq.3, f32[512]{0:T(512)S(1)} %bitcast.43, f32[512,3072]{1,0:T(8,128)} %get-tuple-element.4, s32[]{:T(128)S(6)} %select_n.24, f32[512]{0:T(512)S(1)} %bitcast.41, ...), kind=kLoop, calls=%fused_computation.25 | loop fusion | flops 3932160 | bytes 4727813 | tf_op jit(solution)/shard_map/broadcast_in_dim | solution.py:50
  76.1 78.4 %reduce-scatter.3.cloned.1.call-done = bf16[192,3072]{1,0:T(8,128)(2,1)} async-done(((bf16[768,3072]{1,0:T(8,128)(2,1)}), bf16[192,3072]{1,0:T(8,128)(2,1)}) %reduce-scatter.3.cloned.1.call-update) | async-done | bytes 1179664 | tf_op jit(solution)/shard_map/reduce_scatter | solution.py:41
  (7 shorter events, 0.1 us)
Async XLA Ops:
  7.2 2.8 %copy-start = (bf16[1,512,3072]{2,1,0:T(8,128)(2,1)S(1)}, bf16[1,512,3072]{2,1,0:T(8,128)(2,1)}, u32[]{:S(2)}) copy-start(bf16[1,512,3072]{2,1,0:T(8,128)(2,1)} %param.7) | copy-start | bytes 9437188
  7.2 3.8 %copy-start.2 = (f32[1,3072]{1,0:T(1,128)S(1)}, f32[1,3072]{1,0:T(1,128)}, u32[]{:S(2)}) copy-start(f32[1,3072]{1,0:T(1,128)} %param.9) | copy-start | bytes 36868
  7.2 59.1 %reduce-scatter.5.cloned.1.call-start = ((), (), s32[]{:S(2)}) async-start(), calls=%async_computation.3 | async-start | bytes 3932160 | tf_op jit(solution)/shard_map/reduce_scatter | solution.py:32
  7.2 3.7 %copy-start.3 = (bf16[1,512,768]{2,1,0:T(8,128)(2,1)S(1)}, bf16[1,512,768]{2,1,0:T(8,128)(2,1)}, u32[]{:S(2)}) copy-start(bf16[1,512,768]{2,1,0:T(8,128)(2,1)} %param.6) | copy-start | bytes 2359300
  19.3 135.2 %reduce-scatter.3.cloned.1.call-start = ((), (), s32[]{:S(2)}) async-start(), calls=%async_computation.2 | async-start | bytes 5898240 | tf_op jit(solution)/shard_map/reduce_scatter | solution.py:41
  66.3 6.6 %copy-start.1 = (bf16[512,768]{1,0:T(8,128)(2,1)S(1)}, bf16[512,768]{1,0:T(8,128)(2,1)}, u32[]{:S(2)}) copy-start(bf16[512,768]{1,0:T(8,128)(2,1)} %reduce-scatter.5.cloned.1.call-done) | copy-start | bytes 2359300
  68.7 4.2 %collective-permute-start = (bf16[512,768]{1,0:T(8,128)(2,1)S(1)}, bf16[512,768]{1,0:T(8,128)(2,1)S(1)}, u32[]{:S(2)}, u32[]{:S(2)}) collective-permute-start(bf16[512,768]{1,0:T(8,128)(2,1)S(1)} %add_convert_fusion.1), channel_id=1, source_target_pairs={{16,0},{17,1},{18,2},{19,3},{20,4},{21,5},{22,6},{23,7},{24,8},{25... | collective-permute-start | bytes 2359304 | tf_op jit(solution)/shard_map/ppermute | solution.py:47
Sparse Core Ops, SparseCore 0:
  19.4 46.8 reduce-scatter.4
  69.2 85.2 reduce-scatter.2

commit v2 on v1

v2 whole, which is shorter than its diff:
```python
import functools

import jax
import jax.numpy as jnp
from jax import lax
from jax.experimental import pallas as pl
from jax.experimental.pallas import tpu as pltpu
from jax.sharding import PartitionSpec as P

MESH = pl.DeviceIdType.MESH
TOK_MB = 256
CHUNK = 512
F32, BF16 = jnp.float32, jnp.bfloat16


def kernel(
    n, m, vgt, vg, x, w_hbm, gain, top_hbm, wg, res,
    w, top, normed, stats, own, from_left, from_right, psend, precv, acc1, acc2, ssend, srecv, above, below,
    local_sem, right_send, right_recv, left_send, left_recv, p_send, p_recv, s_send, s_recv, sec_send, sec_recv,
):
    sec, me, r = lax.axis_index("section"), lax.axis_index("mp"), lax.axis_index("dp")
    tokens, width = x.shape
    share = width // m
    chunks = width // CHUNK
    rows_mp = min(128, tokens)
    my_cols = pl.ds(pl.multiple_of(me * share, 128), share)

    load_w = pltpu.make_async_copy(w_hbm, w, local_sem.at[0])
    load_top = pltpu.make_async_copy(top_hbm.at[:, my_cols], top, local_sem.at[1])
    load_w.start()
    load_top.start()

    barrier = pltpu.get_barrier_semaphore()
    for k in range(1, m):
        pl.semaphore_signal(barrier, inc=1, device_id={"mp": lax.rem(me + k, m)}, device_id_type=MESH)
    pl.semaphore_signal(barrier, inc=1, device_id={"section": 1 - sec}, device_id_type=MESH)

    @pl.when(r > 0)
    def _():
        pl.semaphore_signal(barrier, inc=1, device_id={"dp": r - 1}, device_id_type=MESH)

    @pl.when(r < n - 1)
    def _():
        pl.semaphore_signal(barrier, inc=1, device_id={"dp": r + 1}, device_id_type=MESH)

    lane = lambda rows: lax.broadcasted_iota(jnp.int32, (rows, 128), 1)

    def norm_tile(i, _):
        rows = pl.ds(pl.multiple_of(i * 16, 16), 16)
        values = x[rows, :].astype(F32)
        average = jnp.sum(values, axis=-1, keepdims=True) * (1.0 / width)
        centred = values - average
        variance = jnp.sum(centred * centred, axis=-1, keepdims=True) * (1.0 / width)
        inv = lax.rsqrt(variance + 1e-06)
        normed[rows, :] = (centred * inv * gain[...]).astype(BF16)
        stats[rows, :] = jnp.where(lane(16) == 0, average, inv)
        return 0

    lax.fori_loop(0, tokens // 16, norm_tile, 0)

    pl.semaphore_wait(barrier, m + jnp.where(r > 0, 1, 0) + jnp.where(r < n - 1, 1, 0))

    def right_copy(c, b, source):
        return pltpu.make_async_remote_copy(
            src_ref=source.at[c, b], dst_ref=from_left.at[c, b], send_sem=right_send.at[c, b],
            recv_sem=right_recv.at[c, b], device_id={"dp": lax.rem(r + 1, n)}, device_id_type=MESH,
        )

    def left_copy(c, b, source):
        return pltpu.make_async_remote_copy(
            src_ref=source.at[c, b], dst_ref=from_right.at[c, b], send_sem=left_send.at[c, b],
            recv_sem=left_recv.at[c, b], device_id={"dp": lax.rem(r + n - 1, n)}, device_id_type=MESH,
        )

    def product(c):
        def block(i, _):
            b = jnp.where(r == 0, n - 1 - i, i)
            own[c, b] = jnp.dot(
                vgt[b], normed[:, c * CHUNK:(c + 1) * CHUNK], preferred_element_type=F32
            ).astype(BF16)

            @pl.when((r == 0) & (b > 0))
            def _():
                right_copy(c, b, own).start()

            @pl.when((r == n - 1) & (b < n - 1))
            def _():
                left_copy(c, b, own).start()

            return 0

        lax.fori_loop(0, n, block, 0)

    def peer(k):
        return {"mp": lax.rem(me + k, m)}

    def part_copy(k):
        return pltpu.make_async_remote_copy(
            src_ref=psend.at[k], dst_ref=precv.at[k], send_sem=p_send.at[k], recv_sem=p_recv.at[k],
            device_id=peer(k), device_id_type=MESH,
        )

    def sum_copy(k):
        return pltpu.make_async_remote_copy(
            src_ref=ssend, dst_ref=srecv.at[k], send_sem=s_send.at[k], recv_sem=s_recv.at[k],
            device_id=peer(k), device_id_type=MESH,
        )

    def fold(value):
        total = value[:, :128]
        for start in range(128, value.shape[1], 128):
            total = total + value[:, start:start + 128]
        return total

    def whitened_of(rows, cols):
        return (x[rows, cols].astype(F32) - stats[rows, 0:1]) * stats[rows, 1:2]

    def partials():
        load_w.wait()
        for step in range(m):
            k = (step + 1) % m
            cols = pl.ds(pl.multiple_of(lax.rem(me + k, m) * share, 128), share)

            def tile(i, _):
                rows = pl.ds(pl.multiple_of(i * rows_mp, rows_mp), rows_mp)
                part = jnp.dot(vg[rows, :], w[:, cols], preferred_element_type=F32)
                psend[k, rows, :] = part.astype(BF16)
                scaled = part * gain[:, cols]
                first, second = fold(scaled), fold(scaled * whitened_of(rows, cols))
                if step == 0:
                    acc1[rows, :] = first
                    acc2[rows, :] = second
                elif step < m - 1:
                    acc1[rows, :] += first
                    acc2[rows, :] += second
                else:
                    one = jnp.sum(acc1[rows, :] + first, axis=-1, keepdims=True)
                    two = jnp.sum(acc2[rows, :] + second, axis=-1, keepdims=True)
                    ssend[rows, :] = jnp.where(lane(rows_mp) == 0, one, two)
                return 0

            lax.fori_loop(0, tokens // rows_mp, tile, 0)
            if k > 0:
                part_copy(k).start()
        for k in range(1, m):
            sum_copy(k).start()

    def section_copy():
        return pltpu.make_async_remote_copy(
            src_ref=above, dst_ref=below, send_sem=sec_send, recv_sem=sec_recv,
            device_id={"section": 1 - sec}, device_id_type=MESH,
        )

    def residual(base, extra):
        def tile(i, _):
            rows = pl.ds(pl.multiple_of(i * 64, 64), 64)
            grad = psend[0, rows, :].astype(F32)
            sums = ssend[rows, :]
            for k in range(1, m):
                grad = grad + precv[k, rows, :].astype(F32)
                sums = sums + srecv[k, rows, :]
            sums = sums * (1.0 / width)
            scaled = grad * gain[:, my_cols]
            white = whitened_of(rows, my_cols)
            branch = stats[rows, 1:2] * (scaled - sums[:, 0:1] - white * sums[:, 1:2])
            value = (base[rows, :].astype(F32) + branch).astype(BF16)
            res[rows, :] = value
            if extra is not None:
                extra[rows, :] = value
            return 0

        lax.fori_loop(0, tokens // 64, tile, 0)

    def finish_later():
        load_top.wait()
        for k in range(1, m):
            part_copy(k).wait_recv()
            sum_copy(k).wait_recv()

        @pl.when(sec == 1)
        def _():
            residual(top, above)
            section_copy().start()

    def finish_earlier():
        @pl.when(sec == 0)
        def _():
            section_copy().wait_recv()
            residual(below, None)

    def forward(c):
        middle = (r > 0) & (r < n - 1)

        def go_right(i, _):
            b = n - 1 - i
            right_copy(c, b, from_left).wait_recv()
            from_left[c, b] = (from_left[c, b].astype(F32) + own[c, b].astype(F32)).astype(BF16)
            right_copy(c, b, from_left).start()
            return 0

        def go_left(b, _):
            left_copy(c, b, from_right).wait_recv()
            from_right[c, b] = (from_right[c, b].astype(F32) + own[c, b].astype(F32)).astype(BF16)
            left_copy(c, b, from_right).start()
            return 0

        def both(right_first):
            steps = [
                lambda: lax.fori_loop(0, n - 1 - r, go_right, 0),
                lambda: lax.fori_loop(0, r, go_left, 0),
            ]
            for step in steps if right_first else steps[::-1]:
                step()

        @pl.when(middle & (r < n // 2))
        def _():
            both(True)

        @pl.when(middle & (r >= n // 2))
        def _():
            both(False)

    def settle(c):
        cols = slice(c * CHUNK, (c + 1) * CHUNK)

        @pl.when(r == 0)
        def _():
            left_copy(c, r, own).wait_recv()
            wg[:, cols] = (own[c, r].astype(F32) + from_right[c, r].astype(F32)).astype(BF16)

        @pl.when(r == n - 1)
        def _():
            right_copy(c, r, own).wait_recv()
            wg[:, cols] = (own[c, r].astype(F32) + from_left[c, r].astype(F32)).astype(BF16)

        @pl.when((r > 0) & (r < n - 1))
        def _():
            left_copy(c, r, own).wait_recv()
            right_copy(c, r, own).wait_recv()
            wg[:, cols] = (
                own[c, r].astype(F32) + from_left[c, r].astype(F32) + from_right[c, r].astype(F32)
            ).astype(BF16)

    product(0)
    partials()
    for c in range(1, chunks):
        product(c)
    later, earlier = max(chunks - 3, 0), max(chunks - 2, 0)
    for c in range(chunks):
        forward(c)
        settle(c)
        if c == later:
            finish_later()
        if c == earlier:
            finish_earlier()

    for k in range(1, m):
        part_copy(k).wait_send()
        sum_copy(k).wait_send()

    @pl.when(sec == 1)
    def _():
        section_copy().wait_send()

    for c in range(chunks):
        def sent_right(b, _):
            right_copy(c, b, own).wait_send()
            return 0

        def sent_left(b, _):
            left_copy(c, b, own).wait_send()
            return 0

        lax.fori_loop(r + 1, n, sent_right, 0)
        lax.fori_loop(0, r, sent_left, 0)


def solution(mesh):
    n, m = mesh.shape["dp"], mesh.shape["mp"]

    def step(value_grad, stream, weights, gain, top_grad, counts):
        tokens, features = value_grad.shape[1:]
        width = stream.shape[2]
        share, block, chunks = width // m, features // n, width // CHUNK
        micro = jnp.arange(tokens, dtype=jnp.int32) // TOK_MB
        live = (micro < counts[0]).astype(BF16)
        turned = (value_grad[0] * live[:, None]).T.reshape(n, block, tokens)
        vmem = pl.BlockSpec(memory_space=pltpu.VMEM)
        hbm = pl.BlockSpec(memory_space=pl.ANY)
        dma = pltpu.SemaphoreType.DMA
        chain = (chunks, n, block, CHUNK)
        wg, res = pl.pallas_call(
            functools.partial(kernel, n, m),
            out_shape=(
                jax.ShapeDtypeStruct((block, width), BF16),
                jax.ShapeDtypeStruct((tokens, share), BF16),
            ),
            in_specs=[vmem, vmem, vmem, hbm, vmem, hbm],
            out_specs=(vmem, vmem),
            scratch_shapes=[
                pltpu.VMEM((features, width), BF16),
                pltpu.VMEM((tokens, share), BF16),
                pltpu.VMEM((tokens, width), BF16),
                pltpu.VMEM((tokens, 128), F32),
                pltpu.VMEM(chain, BF16),
                pltpu.VMEM(chain, BF16),
                pltpu.VMEM(chain, BF16),
                pltpu.VMEM((m, tokens, share), BF16),
                pltpu.VMEM((m, tokens, share), BF16),
                pltpu.VMEM((tokens, 128), F32),
                pltpu.VMEM((tokens, 128), F32),
                pltpu.VMEM((tokens, 128), F32),
                pltpu.VMEM((m, tokens, 128), F32),
                pltpu.VMEM((tokens, share), BF16),
                pltpu.VMEM((tokens, share), BF16),
                dma((2,)),
                dma((chunks, n)), dma((chunks, n)), dma((chunks, n)), dma((chunks, n)),
                dma((m,)), dma((m,)), dma((m,)), dma((m,)),
                dma, dma,
            ],
            compiler_params=pltpu.CompilerParams(
                collective_id=0, has_side_effects=True, vmem_limit_bytes=56 * 2**20
            ),
        )(turned, value_grad[0], stream[0], weights[0], gain, top_grad)
        return wg[None], res[None]

    in_specs = (
        P("section", "dp", "mp"),
        P("section", "dp", None),
        P("section", "mp", None),
        P("section", None),
        P("dp", None),
        P("dp"),
    )
    out_specs = (P("section", ("mp", "dp"), None), P("section", "dp", "mp"))
    return jax.shard_map(step, mesh=mesh, in_specs=in_specs, out_specs=out_specs, check_vma=False)
```

time: 162 us -> 104 us (0.64)
  waiting for transfers between devices: 110 us -> 0 us
  Pallas kernels: 0 us -> 95.5 us
  matrix products: 14.2 us -> 0 us
  between operations: 14.8 us -> 1.3 us
  blocking collectives: 11.9 us -> 0 us
  other arithmetic: 9.15 us -> 1.28 us
  local copies, waits for them, and re-layouts: 0.27 us -> 5.58 us
    reduce_scatter x2 -> x0, waiting for transfers between devices: 107 us -> none  [the longest x1 78.4 us: shards(): lax.psum_scatter(product.astype(jnp.bfloat16), 'dp', scatter_dimension=0,...]
    pallas_call x0 -> x1, Pallas kernels: none -> 95.5 us  [step(): pl.pallas_call(functools.partial(kernel, n, m), out_shape=(jax.ShapeDtype...]
    dot_general x2 -> x0, matrix products: 14.2 us -> none  [the longest x1 8.28 us: shards(): jnp.dot(value_grad[0], weights[0], preferred_element_type=jnp.float32)]
    psum x1 -> x0, blocking collectives: 11.9 us -> none  [shards(): sums = lax.psum(sums, 'mp') * (1.0 / width)]
    unnamed x8 -> x2, local copies, waits for them, and re-layouts: 0.24 us -> 4.42 us
    reduce_sum x2 -> x0, other arithmetic: 3.48 us -> none  [the longest x1 2.53 us: normalize(): average = jnp.mean(values, axis=-1, keepdims=True)]
    broadcast_in_dim x1 -> x0, other arithmetic: 3.23 us -> none  [shards(): return (weight_grad, result[None])]
    ppermute x1 -> x0, waiting for transfers between devices: 2.87 us -> none  [shards(): below = lax.ppermute(above, 'section', [(1, 0)])]
  transfers between devices with their start and end apart: 3 -> 0, of which waited for: 3 -> 0; matrix products, arithmetic and copies ran while one was open for 7% -> 0% of each run, Pallas kernels for 0% -> 0%
where the time goes in v2:
time: 104 us
  Pallas kernels  95.5 us (92%)
  local copies, waits for them, and re-layouts  5.58 us (5%)
  between operations  1.3 us (1%)
  other arithmetic  1.28 us (1%)
    pallas_call x1, Pallas kernels, step(): pl.pallas_call(functools.partial(kernel, n, m), out_shape=(jax.ShapeDtype...  95.5 us
    unnamed x2, local copies, waits for them, and re-layouts  4.42 us

profile of v2, /device:TPU:0, one launch (start us, length us, event | category | flops | bytes accessed | tf_op | source)
XLA Modules:
  0.0 103.6 jit_solution(1023518942881348066)
XLA Ops:
  1.3 1.3 %multiply_bitcast_fusion = bf16[768,512]{0,1:T(8,128)(2,1)S(1)} fusion(bf16[512]{0:T(512)(128)(2,1)S(1)} %fusion.4, bf16[1,512,768]{2,1,0:T(8,128)(2,1)} %param.6), kind=kLoop, calls=%fused_computation | loop fusion | flops 393216 | bytes 1573888 | tf_op jit(solution)/shard_map/transpose | solution.py:287
  2.6 1.2 %copy.9 = bf16[768,512]{1,0:T(8,128)(2,1)} copy(bf16[768,512]{0,1:T(8,128)(2,1)S(1)} %multiply_bitcast_fusion) | data formatting | bytes 1572864 | tf_op jit(solution)/shard_map/transpose | solution.py:287
  3.7 95.5 %shard_map.77 = (bf16[192,3072]{1,0:T(8,128)(2,1)}, bf16[512,768]{1,0:T(8,128)(2,1)}) custom-call(bf16[4,192,512]{2,1,0:T(8,128)(2,1)} %bitcast.12, bf16[512,768]{1,0:T(8,128)(2,1)} %bitcast.13, bf16[512,3072]{1,0:T(8,128)(2,1)} %bitcast.14, bf16[768,3072]{1,0:T(8,128)(2,1)} %bitcast.11, f32[1,3072]{1,0:T(1,128)} %gain.1, bf16[512,3072]{1,0:T(8,128)(2,1)} %top_hbm.1), custom_call_target="tpu_custom_call" | custom-call | tf_op jit(solution)/shard_map/pallas_call | solution.py:292
  99.2 2.4 %copy.13 = bf16[1,192,3072]{2,1,0:T(8,128)(2,1)} copy(bf16[1,192,3072]{2,1,0:T(8,128)(2,1)} %bitcast.15) | data formatting | bytes 2359296
  101.6 2.1 %copy.14 = bf16[1,512,768]{2,1,0:T(8,128)(2,1)} copy(bf16[1,512,768]{2,1,0:T(8,128)(2,1)} %bitcast.16) | data formatting | bytes 1572864
  (1 shorter events, 0.0 us)

commit v3 on v2

--- a/solution.py
+++ b/solution.py
@@ -14,8 +14,8 @@
 
 
 def kernel(
-    n, m, vgt, vg, x, w_hbm, gain, top_hbm, wg, res,
-    w, top, normed, stats, own, from_left, from_right, psend, precv, acc1, acc2, ssend, srecv, above, below,
+    n, m, live, vg, x, w_hbm, gain, top_hbm, wg, res,
+    w, top, vgt, normed, stats, own, from_left, from_right, psend, precv, acc1, acc2, ssend, srecv, above, below,
     local_sem, right_send, right_recv, left_send, left_recv, p_send, p_recv, s_send, s_recv, sec_send, sec_recv,
 ):
     sec, me, r = lax.axis_index("section"), lax.axis_index("mp"), lax.axis_index("dp")
@@ -56,7 +56,10 @@
         stats[rows, :] = jnp.where(lane(16) == 0, average, inv)
         return 0
 
-    lax.fori_loop(0, tokens // 16, norm_tile, 0)
+    lax.fori_loop(0, tokens // 16, norm_tile, 0, unroll=2)
+
+    features = vg.shape[1]
+    vgt[...] = (vg[...].T * live[...]).reshape(n, features // n, tokens)
 
     pl.semaphore_wait(barrier, m + jnp.where(r > 0, 1, 0) + jnp.where(r < n - 1, 1, 0))
 
@@ -275,6 +278,27 @@
         lax.fori_loop(0, r, sent_left, 0)
 
 
+def pass_kernel(wg_in, res_in, wg_out, res_out):
+    wg_out[...] = wg_in[...]
+    res_out[...] = res_in[...]
+
+
+def passed_on(wg, res):
+    steps = 4
+    specs = [
+        pl.BlockSpec((wg.shape[0], wg.shape[1] // steps), lambda i: (0, i)),
+        pl.BlockSpec((res.shape[0] // steps, res.shape[1]), lambda i: (i, 0)),
+    ]
+    return pl.pallas_call(
+        pass_kernel,
+        grid=(steps,),
+        out_shape=(jax.ShapeDtypeStruct(wg.shape, wg.dtype), jax.ShapeDtypeStruct(res.shape, res.dtype)),
+        in_specs=specs,
+        out_specs=tuple(specs),
+        compiler_params=pltpu.CompilerParams(vmem_limit_bytes=8 * 2**20),
+    )(wg, res)
+
+
 def solution(mesh):
     n, m = mesh.shape["dp"], mesh.shape["mp"]
 
@@ -284,7 +308,6 @@
         share, block, chunks = width // m, features // n, width // CHUNK
         micro = jnp.arange(tokens, dtype=jnp.int32) // TOK_MB
         live = (micro < counts[0]).astype(BF16)
-        turned = (value_grad[0] * live[:, None]).T.reshape(n, block, tokens)
         vmem = pl.BlockSpec(memory_space=pltpu.VMEM)
         hbm = pl.BlockSpec(memory_space=pl.ANY)
         dma = pltpu.SemaphoreType.DMA
@@ -300,6 +323,7 @@
             scratch_shapes=[
                 pltpu.VMEM((features, width), BF16),
                 pltpu.VMEM((tokens, share), BF16),
+                pltpu.VMEM((n, block, tokens), BF16),
                 pltpu.VMEM((tokens, width), BF16),
                 pltpu.VMEM((tokens, 128), F32),
                 pltpu.VMEM(chain, BF16),
@@ -319,10 +343,10 @@
                 dma, dma,
             ],
             compiler_params=pltpu.CompilerParams(
-                collective_id=0, has_side_effects=True, vmem_limit_bytes=56 * 2**20
+                collective_id=0, has_side_effects=True, vmem_limit_bytes=46 * 2**20
             ),
-        )(turned, value_grad[0], stream[0], weights[0], gain, top_grad)
-        return wg[None], res[None]
+        )(live[None, :], value_grad[0], stream[0], weights[0], gain, top_grad)
+        return tuple(a[None] for a in passed_on(wg, res))
 
     in_specs = (
         P("section", "dp", "mp"),

time: 104 us -> 96 us (0.923)
  Pallas kernels: 95.5 us -> 90.7 us
  local copies, waits for them, and re-layouts: 5.58 us -> 3.72 us
  other arithmetic: 1.28 us -> 0.01 us
    pallas_call x1, Pallas kernels: 95.5 us -> 88.9 us  [step(): pl.pallas_call(functools.partial(kernel, n, m), out_shape=(jax.ShapeDtype...]
    pallas_call x0 -> x1, Pallas kernels: none -> 1.87 us  [passed_on(): pl.pallas_call(pass_kernel, grid=(steps,), out_shape=(jax.ShapeDtypeStruc...]
    transpose x1 -> x0, other arithmetic: 1.27 us -> none  [step(): turned = (value_grad[0] * live[:, None]).T.reshape(n, block, tokens)]
    transpose x1 -> x0, local copies, waits for them, and re-layouts: 1.16 us -> none  [step(): turned = (value_grad[0] * live[:, None]).T.reshape(n, block, tokens)]
    unnamed x2 -> x6, local copies, waits for them, and re-layouts: 4.42 us -> 3.72 us
where the time goes in v3:
time: 96 us; the launch traced here: 95.8 us
  Pallas kernels  90.7 us (94%)
  local copies, waits for them, and re-layouts  3.72 us (4%)
  between operations  1.3 us (1%)
    pallas_call x1, Pallas kernels, step(): pl.pallas_call(functools.partial(kernel, n, m), out_shape=(jax.ShapeDtype...  88.9 us
    unnamed x6, local copies, waits for them, and re-layouts  3.72 us

profile of v3, /device:TPU:0, one launch (start us, length us, event | category | flops | bytes accessed | tf_op | source)
XLA Modules:
  0.0 95.8 jit_solution(9379015578969825051)
XLA Ops:
  1.3 0.0 copy-start
  1.3 1.9 %copy-done = bf16[1,512,3072]{2,1,0:T(8,128)(2,1)S(1)} copy-done((bf16[1,512,3072]{2,1,0:T(8,128)(2,1)S(1)}, bf16[1,512,3072]{2,1,0:T(8,128)(2,1)}, u32[]{:S(2)}) %copy-start) | copy-done | bytes 3145752
  3.2 0.0 copy-start.1
  3.2 1.1 %copy-done.1 = bf16[1,512,768]{2,1,0:T(8,128)(2,1)S(1)} copy-done((bf16[1,512,768]{2,1,0:T(8,128)(2,1)S(1)}, bf16[1,512,768]{2,1,0:T(8,128)(2,1)}, u32[]{:S(2)}) %copy-start.1) | copy-done | bytes 786456
  4.3 0.0 copy-start.2
  4.3 0.7 copy-done.2
  5.0 88.9 %shard_map.77 = (bf16[192,3072]{1,0:T(8,128)(2,1)S(1)}, bf16[512,768]{1,0:T(8,128)(2,1)S(1)}) custom-call(bf16[1,512]{1,0:T(2,128)(2,1)S(1)} %compare_convert_fusion.live, bf16[512,768]{1,0:T(8,128)(2,1)S(1)} %bitcast.8, bf16[512,3072]{1,0:T(8,128)(2,1)S(1)} %bitcast.7, bf16[768,3072]{1,0:T(8,128)(2,1)} %bitcast.9, f32[1,3072]{1,0:T(1,128)S(1)} %copy-done.2, ...), custom_call_target="tpu_custom_call" | custom-call | tf_op jit(solution)/shard_map/pallas_call | solution.py:315
  93.9 1.9 %shard_map.78 = (bf16[192,3072]{1,0:T(8,128)(2,1)}, bf16[512,768]{1,0:T(8,128)(2,1)}) custom-call(bf16[192,3072]{1,0:T(8,128)(2,1)S(1)} %get-tuple-element.6.wg_in, bf16[512,768]{1,0:T(8,128)(2,1)S(1)} %get-tuple-element.7.res_in), custom_call_target="tpu_custom_call" | custom-call | tf_op jit(solution)/shard_map/pallas_call | solution.py:292
  (1 shorter events, 0.0 us)
Async XLA Ops:
  1.3 1.9 %copy-start = (bf16[1,512,3072]{2,1,0:T(8,128)(2,1)S(1)}, bf16[1,512,3072]{2,1,0:T(8,128)(2,1)}, u32[]{:S(2)}) copy-start(bf16[1,512,3072]{2,1,0:T(8,128)(2,1)} %param.7) | copy-start | bytes 9437188
  3.2 1.1 %copy-start.1 = (bf16[1,512,768]{2,1,0:T(8,128)(2,1)S(1)}, bf16[1,512,768]{2,1,0:T(8,128)(2,1)}, u32[]{:S(2)}) copy-start(bf16[1,512,768]{2,1,0:T(8,128)(2,1)} %param.6) | copy-start | bytes 2359300
  4.3 0.7 copy-start.2

commit v4 on v3

--- a/solution.py
+++ b/solution.py
@@ -10,12 +10,13 @@
 MESH = pl.DeviceIdType.MESH
 TOK_MB = 256
 CHUNK = 512
+PIECES = 4
 F32, BF16 = jnp.float32, jnp.bfloat16
 
 
 def kernel(
-    n, m, live, vg, x, w_hbm, gain, top_hbm, wg, res,
-    w, top, vgt, normed, stats, own, from_left, from_right, psend, precv, acc1, acc2, ssend, srecv, above, below,
+    n, m, live, vg_hbm, x_hbm, w_hbm, gain_hbm, top_hbm, wg, res,
+    vg, x, gain, w, top, vgt, normed, stats, own, from_left, from_right, psend, precv, acc1, acc2, ssend, srecv, above, below,
     local_sem, right_send, right_recv, left_send, left_recv, p_send, p_recv, s_send, s_recv, sec_send, sec_recv,
 ):
     sec, me, r = lax.axis_index("section"), lax.axis_index("mp"), lax.axis_index("dp")
@@ -27,6 +28,18 @@
 
     load_w = pltpu.make_async_copy(w_hbm, w, local_sem.at[0])
     load_top = pltpu.make_async_copy(top_hbm.at[:, my_cols], top, local_sem.at[1])
+    load_gain = pltpu.make_async_copy(gain_hbm, gain, local_sem.at[2])
+    load_vg = pltpu.make_async_copy(vg_hbm, vg, local_sem.at[3])
+    piece = tokens // PIECES
+
+    def load_x(p):
+        rows = pl.ds(p * piece, piece)
+        return pltpu.make_async_copy(x_hbm.at[rows, :], x.at[rows, :], local_sem.at[4 + p])
+
+    load_gain.start()
+    for p in range(PIECES):
+        load_x(p).start()
+    load_vg.start()
     load_w.start()
     load_top.start()
 
@@ -56,7 +69,11 @@
         stats[rows, :] = jnp.where(lane(16) == 0, average, inv)
         return 0
 
-    lax.fori_loop(0, tokens // 16, norm_tile, 0, unroll=2)
+    load_gain.wait()
+    for p in range(PIECES):
+        load_x(p).wait()
+        lax.fori_loop(p * (piece // 16), (p + 1) * (piece // 16), norm_tile, 0, unroll=2)
+    load_vg.wait()
 
     features = vg.shape[1]
     vgt[...] = (vg[...].T * live[...]).reshape(n, features // n, tokens)
@@ -295,7 +312,7 @@
         out_shape=(jax.ShapeDtypeStruct(wg.shape, wg.dtype), jax.ShapeDtypeStruct(res.shape, res.dtype)),
         in_specs=specs,
         out_specs=tuple(specs),
-        compiler_params=pltpu.CompilerParams(vmem_limit_bytes=8 * 2**20),
+        compiler_params=pltpu.CompilerParams(vmem_limit_bytes=60 * 2**20),
     )(wg, res)
 
 
@@ -309,7 +326,7 @@
         micro = jnp.arange(tokens, dtype=jnp.int32) // TOK_MB
         live = (micro < counts[0]).astype(BF16)
         vmem = pl.BlockSpec(memory_space=pltpu.VMEM)
-        hbm = pl.BlockSpec(memory_space=pl.ANY)
+        hbm = pl.BlockSpec(memory_space=pltpu.HBM)
         dma = pltpu.SemaphoreType.DMA
         chain = (chunks, n, block, CHUNK)
         wg, res = pl.pallas_call(
@@ -318,9 +335,12 @@
                 jax.ShapeDtypeStruct((block, width), BF16),
                 jax.ShapeDtypeStruct((tokens, share), BF16),
             ),
-            in_specs=[vmem, vmem, vmem, hbm, vmem, hbm],
+            in_specs=[vmem, hbm, hbm, hbm, hbm, hbm],
             out_specs=(vmem, vmem),
             scratch_shapes=[
+                pltpu.VMEM((tokens, features), BF16),
+                pltpu.VMEM((tokens, width), BF16),
+                pltpu.VMEM((1, width), F32),
                 pltpu.VMEM((features, width), BF16),
                 pltpu.VMEM((tokens, share), BF16),
                 pltpu.VMEM((n, block, tokens), BF16),
@@ -337,13 +357,13 @@
                 pltpu.VMEM((m, tokens, 128), F32),
                 pltpu.VMEM((tokens, share), BF16),
                 pltpu.VMEM((tokens, share), BF16),
-                dma((2,)),
+                dma((4 + PIECES,)),
                 dma((chunks, n)), dma((chunks, n)), dma((chunks, n)), dma((chunks, n)),
                 dma((m,)), dma((m,)), dma((m,)), dma((m,)),
                 dma, dma,
             ],
             compiler_params=pltpu.CompilerParams(
-                collective_id=0, has_side_effects=True, vmem_limit_bytes=46 * 2**20
+                collective_id=0, has_side_effects=True, vmem_limit_bytes=60 * 2**20
             ),
         )(live[None, :], value_grad[0], stream[0], weights[0], gain, top_grad)
         return tuple(a[None] for a in passed_on(wg, res))

time: 96 us -> 97.7 us (1.018)
  Pallas kernels: 90.7 us -> 95.6 us
  local copies, waits for them, and re-layouts: 3.72 us -> 0 us
    unnamed x6 -> x0, local copies, waits for them, and re-layouts: 3.72 us -> none
    pallas_call x1, Pallas kernels: 88.9 us -> 91.9 us  [step(): pl.pallas_call(functools.partial(kernel, n, m), out_shape=(jax.ShapeDtype...]
    pallas_call x1, Pallas kernels: 1.87 us -> 3.69 us  [passed_on(): pl.pallas_call(pass_kernel, grid=(steps,), out_shape=(jax.ShapeDtypeStruc...]
where the time goes in v4:
time: 97.7 us; the launch traced here: 97.5 us
  Pallas kernels  95.6 us (98%)
  between operations  1.28 us (1%)
    pallas_call x1, Pallas kernels, step(): pl.pallas_call(functools.partial(kernel, n, m), out_shape=(jax.ShapeDtype...  91.9 us
    pallas_call x1, Pallas kernels, passed_on(): pl.pallas_call(pass_kernel, grid=(steps,), out_shape=(jax.ShapeDtypeStruc...  3.69 us

profile of v4, /device:TPU:0, one launch (start us, length us, event | category | flops | bytes accessed | tf_op | source)
XLA Modules:
  0.0 97.5 jit_solution(481404144057135925)
XLA Ops:
  1.3 0.6 compare_convert_fusion.live
  1.9 91.9 %shard_map.77 = (bf16[192,3072]{1,0:T(8,128)(2,1)}, bf16[512,768]{1,0:T(8,128)(2,1)}) custom-call(bf16[1,512]{1,0:T(2,128)(2,1)} %compare_convert_fusion.live, bf16[512,768]{1,0:T(8,128)(2,1)} %bitcast.9, bf16[512,3072]{1,0:T(8,128)(2,1)} %bitcast.8, bf16[768,3072]{1,0:T(8,128)(2,1)} %bitcast.7, f32[1,3072]{1,0:T(1,128)} %gain_hbm.1, bf16[512,3072]{1,0:T(8,128)(2,1)} %top_hbm.1), custom_call_target="tpu_custom_call" | custom-call | tf_op jit(solution)/shard_map/pallas_call | solution.py:332
  93.8 3.7 %shard_map.78 = (bf16[192,3072]{1,0:T(8,128)(2,1)}, bf16[512,768]{1,0:T(8,128)(2,1)}) custom-call(bf16[192,3072]{1,0:T(8,128)(2,1)} %get-tuple-element.6.wg_in, bf16[512,768]{1,0:T(8,128)(2,1)} %get-tuple-element.7.res_in), custom_call_target="tpu_custom_call" | custom-call | tf_op jit(solution)/shard_map/pallas_call | solution.py:309
